TPU v7x, 128 devices: a whole 4x4x4 slice. The times are simulated.
128 devices in a mesh: dp: 64 (over z_hi, x, y, core), mp: 2 (over z_lo).
Axes of the slice: x: 4, y: 4, z: 4 (z_hi: 2, z_lo: 2; z = z_hi * 2 + z_lo), core: 2. Of those that a mesh axis runs over, the one named last changes fastest.
Arguments:
- inputs: bfloat16 [8192, 1792], P('dp', 'mp'), may hold values from -6 to 6
- cotangent: bfloat16 [8192, 1792], P('dp', 'mp'), may hold values from -6 to 6
- gate_weight: bfloat16 [9472, 1792], P(('mp', 'dp')), may hold values from -0.125 to 0.125
- up_weight: bfloat16 [9472, 1792], P(('mp', 'dp')), may hold values from -0.125 to 0.125
- down_weight: bfloat16 [9472, 1792], P(('mp', 'dp')), may hold values from -0.0625 to 0.0625
Outputs:
- input_grad: bfloat16 [8192, 1792], P('dp', 'mp')
- gate_grad: bfloat16 [9472, 1792], P(('mp', 'dp'))
All inputs are finite; a program needn't handle non-finite values.
Results may differ from a plain program's by a relative error of at most 0.009.
Values may be sent and summed in bfloat16 or wider, within the bound.
A program may use at most 320 MiB of HBM per device.

v0:
```python
import jax
import jax.numpy as jnp
from jax import lax
from jax.sharding import Mesh
from jax.sharding import PartitionSpec as P

DP = ("dp_0", "dp_1", "dp_2", "dp_3")
MP_DP = ("mp", "dp_0", "dp_1", "dp_2", "dp_3")
TOK = ("dp_0", "dp_1", "mp")
HID = ("dp_2", "dp_3")


def tdot(left, right):
    return lax.dot_general(
        left, right, (((0,), (0,)), ((), ())), preferred_element_type=jnp.float32
    )


def rdot(left, right):
    return lax.dot_general(
        left, right, (((1,), (1,)), ((), ())), preferred_element_type=jnp.float32
    )


def whole_rows(pieces):
    groups, rows, width = pieces.shape
    halves = pieces.reshape(groups // 2, 2, rows, width)
    return jnp.moveaxis(halves, 1, 2).reshape(groups // 2 * rows, 2 * width)


def per_device(inputs, cotangent, gate_weight, up_weight, down_weight):
    rows, half = inputs.shape
    full_in = whole_rows(lax.all_gather(inputs, TOK, axis=0))
    full_cot = whole_rows(lax.all_gather(cotangent, TOK, axis=0))
    wg = lax.all_gather(gate_weight, HID, axis=0, tiled=True)
    wu = lax.all_gather(up_weight, HID, axis=0, tiled=True)
    wd = lax.all_gather(down_weight, HID, axis=0, tiled=True)
    gate = rdot(full_in, wg)
    up = rdot(full_in, wu)
    dhidden = rdot(full_cot, wd)
    sig = jax.nn.sigmoid(gate)
    act = gate * sig
    dup = (dhidden * act).astype(jnp.bfloat16)
    dgate = (dhidden * up * sig * (1.0 + gate * (1.0 - sig))).astype(jnp.bfloat16)
    total = jnp.dot(dgate, wg, preferred_element_type=jnp.float32)
    total = total + jnp.dot(dup, wu, preferred_element_type=jnp.float32)
    blocks = total.astype(jnp.bfloat16).reshape(-1, rows, 2, half)
    blocks = jnp.moveaxis(blocks, 2, 1).reshape(-1, rows, half)
    input_grad = lax.psum_scatter(blocks, TOK, scatter_dimension=0)
    gate_sum = tdot(dgate, full_in).astype(jnp.bfloat16)
    gate_grad = lax.psum_scatter(gate_sum, HID, scatter_dimension=0, tiled=True)
    return (input_grad, gate_grad)


def solution(mesh):
    torus = Mesh(
        mesh.devices.reshape(2, 4, 4, 2, mesh.shape["mp"]), ("dp_0", "dp_1", "dp_2", "dp_3", "mp")
    )
    return jax.shard_map(
        per_device,
        mesh=torus,
        in_specs=(P(DP, "mp"), P(DP, "mp"), P(MP_DP, None), P(MP_DP, None), P(MP_DP, None)),
        out_specs=(P(DP, "mp"), P(MP_DP, None)),
        check_vma=False,
    )
```

profile of v0, /device:TPU:2, one launch (start us, length us, event | category | flops | bytes accessed | tf_op | source)
XLA Modules:
  0.0 403.8 jit_solution(16914691176496498846)
XLA Ops:
  7.2 0.7 all-gather.19.cloned.1.call-update
  7.9 0.0 all-gather.17.cloned.1.call-start
  7.9 0.7 all-gather.17.cloned.1.call-update
  8.6 0.0 all-gather.15.cloned.1.call-start
  8.7 0.7 all-gather.15.cloned.1.call-update
  9.4 0.5 all-gather.13.cloned.1.call-update
  10.0 0.5 all-gather.11.cloned.1.call-update
  10.5 0.0 reduce-scatter.4.cloned.1.call-start
  10.6 27.0 %all-gather.19.cloned.1.call-done = bf16[8,74,1792]{2,1,0:T(8,128)(2,1)} async-done(((bf16[1,74,1792]{2,1,0:T(8,128)(2,1)}), bf16[8,74,1792]{2,1,0:T(8,128)(2,1)}) %all-gather.19.cloned.1.call-update) | async-done | bytes 2121744 | tf_op jit(solution)/shard_map/all_gather | solution.py:35
  37.6 1.9 reshape.37
  39.5 25.8 %all-gather.17.cloned.1.call-done = bf16[8,74,1792]{2,1,0:T(8,128)(2,1)} async-done(((bf16[1,74,1792]{2,1,0:T(8,128)(2,1)}), bf16[8,74,1792]{2,1,0:T(8,128)(2,1)}) %all-gather.17.cloned.1.call-update) | async-done | bytes 2121744 | tf_op jit(solution)/shard_map/all_gather | solution.py:36
  65.3 2.9 reshape.35
  68.2 24.8 %all-gather.15.cloned.1.call-done = bf16[8,74,1792]{2,1,0:T(8,128)(2,1)} async-done(((bf16[1,74,1792]{2,1,0:T(8,128)(2,1)}), bf16[8,74,1792]{2,1,0:T(8,128)(2,1)}) %all-gather.15.cloned.1.call-update) | async-done | bytes 2121744 | tf_op jit(solution)/shard_map/all_gather | solution.py:37
  93.0 2.9 reshape.33
  95.9 86.8 %all-gather.13.cloned.1.call-done = bf16[2048,896]{1,0:T(8,128)(2,1)} async-done(((bf16[128,896]{1,0:T(8,128)(2,1)}), bf16[2048,896]{1,0:T(8,128)(2,1)}) %all-gather.13.cloned.1.call-update) | async-done | bytes 3670032 | tf_op jit(solution)/shard_map/all_gather | solution.py:33
  182.6 6.5 %copy.12 = bf16[8,2,128,896]{2,0,3,1:T(8,128)(2,1)} copy(bf16[8,2,128,896]{3,2,1,0:T(8,128)(2,1)} %bitcast.44) | data formatting | bytes 7340032 | tf_op jit(solution)/shard_map/reshape | solution.py:27
  189.1 82.3 %all-gather.11.cloned.1.call-done = bf16[2048,896]{1,0:T(8,128)(2,1)} async-done(((bf16[128,896]{1,0:T(8,128)(2,1)}), bf16[2048,896]{1,0:T(8,128)(2,1)}) %all-gather.11.cloned.1.call-update) | async-done | bytes 3670032 | tf_op jit(solution)/shard_map/all_gather | solution.py:34
  271.5 6.5 %copy.11 = bf16[8,2,128,896]{2,0,3,1:T(8,128)(2,1)} copy(bf16[8,2,128,896]{3,2,1,0:T(8,128)(2,1)} %bitcast.48) | data formatting | bytes 7340032 | tf_op jit(solution)/shard_map/reshape | solution.py:27
  277.9 5.2 %fusion.7 = f32[1024,592]{0,1:T(8,128)S(1)} fusion(bf16[592,1792]{1,0:T(8,128)(2,1)} %reshape.33, bf16[224,8,8,128]{3,2,1,0:T(8,128)(2,1)} %bitcast.49), kind=kOutput, calls=%fused_computation.7 | convolution fusion | flops 2172649472 | bytes 8216576 | tf_op jit(solution)/shard_map/dot_general | solution.py:20
  283.1 2.4 fusion.5
  285.5 2.9 multiply_convert_fusion.1
  288.4 3.1 fusion.20
  291.6 4.9 %add_convert_fusion = bf16[1024,1792]{1,0:T(8,128)(2,1)} fusion(f32[1024,1792]{1,0:T(8,128)S(1)} %fusion.20, bf16[592,1792]{1,0:T(8,128)(2,1)S(1)} %copy-done.1, f32[1024,592]{0,1:T(8,128)S(1)} %fusion.7, f32[1024,592]{0,1:T(8,128)S(1)} %fusion.5), kind=kOutput, calls=%fused_computation | convolution fusion | flops 2179956736 | bytes 17981440 | tf_op jit(solution)/shard_map/dot_general | solution.py:46
  296.5 8.1 %reshape.26 = bf16[8,128,2,896]{3,2,1,0:T(2,128)(2,1)} reshape(bf16[1024,1792]{1,0:T(8,128)(2,1)} %add_convert_fusion) | data formatting | bytes 7340032 | tf_op jit(solution)/shard_map/reshape | solution.py:47
  304.6 4.6 %copy.13 = bf16[8,2,128,896]{3,2,1,0:T(8,128)(2,1)} copy(bf16[8,2,128,896]{3,1,2,0:T(2,128)(2,1)} %bitcast.43) | data formatting | bytes 7340032 | tf_op jit(solution)/shard_map/transpose | solution.py:48
  309.2 4.4 %fusion.10 = bf16[592,1792]{1,0:T(8,128)(2,1)S(1)} fusion(bf16[1024,592]{0,1:T(8,128)(2,1)S(1)} %multiply_convert_fusion.1, bf16[224,8,8,128]{3,2,1,0:T(8,128)(2,1)} %bitcast.45), kind=kOutput, calls=%fused_computation.10 | convolution fusion | flops 2173710336 | bytes 7004160 | tf_op jit(solution)/shard_map/dot_general | solution.py:14
  313.7 23.4 %fusion = bf16[80,1792]{1,0:T(8,128)(2,1)S(1)} fusion(bf16[592,1792]{1,0:T(8,128)(2,1)S(1)} %fusion.10), kind=kCustom, calls=%all-reduce-scatter | all-reduce-scatter fusion | flops 1146881 | bytes 2408960
  337.1 1.3 collective-permute-start
  338.4 0.6 dynamic-slice.4
  339.7 0.9 concatenate
  340.6 0.8 constant_dynamic-slice_fusion
  341.4 55.5 %reduce-scatter.4.cloned.1.call-done = bf16[1,128,896]{2,1,0:T(8,128)(2,1)} async-done(((bf16[16,128,896]{2,1,0:T(8,128)(2,1)}), bf16[1,128,896]{2,1,0:T(8,128)(2,1)}) %reduce-scatter.4.cloned.1.call-update) | async-done | bytes 229392 | tf_op jit(solution)/shard_map/reduce_scatter | solution.py:49
  (12 shorter events, 0.2 us)
Async XLA Ops:
  7.2 30.4 %all-gather.19.cloned.1.call-start = ((), (), s32[]{:S(2)}) async-start(), calls=%async_computation.6 | async-start | bytes 2580480 | tf_op jit(solution)/shard_map/all_gather | solution.py:35
  7.9 57.4 %all-gather.17.cloned.1.call-start = ((), (), s32[]{:S(2)}) async-start(), calls=%async_computation.5 | async-start | bytes 2580480 | tf_op jit(solution)/shard_map/all_gather | solution.py:36
  8.6 84.4 %all-gather.15.cloned.1.call-start = ((), (), s32[]{:S(2)}) async-start(), calls=%async_computation.4 | async-start | bytes 2580480 | tf_op jit(solution)/shard_map/all_gather | solution.py:37
  9.4 173.3 %all-gather.13.cloned.1.call-start = ((), (), s32[]{:S(2)}) async-start(), calls=%async_computation.3 | async-start | bytes 3899392 | tf_op jit(solution)/shard_map/all_gather | solution.py:33
  10.0 261.5 %all-gather.11.cloned.1.call-start = ((), (), s32[]{:S(2)}) async-start(), calls=%async_computation.2 | async-start | bytes 3899392 | tf_op jit(solution)/shard_map/all_gather | solution.py:34
  10.5 386.4 %reduce-scatter.4.cloned.1.call-start = ((), (), s32[]{:S(2)}) async-start(), calls=%async_computation.1 | async-start | bytes 3899392 | tf_op jit(solution)/shard_map/reduce_scatter | solution.py:49
  277.9 5.2 %copy-start = (bf16[8,2,128,896]{2,0,3,1:T(8,128)(2,1)S(1)}, bf16[8,2,128,896]{2,0,3,1:T(8,128)(2,1)}, u32[]{:S(2)}) copy-start(bf16[8,2,128,896]{2,0,3,1:T(8,128)(2,1)} %copy.12) | copy-start | bytes 11010052
  283.1 2.4 copy-start.1
  313.7 24.7 %copy-start.2 = (u32[128]{0:T(128)S(1)}, u32[128]{0:T(128)}, u32[]{:S(2)}) copy-start(u32[128]{0:T(128)} %constant.7) | copy-start | bytes 1540
  337.1 2.6 collective-permute-start
Sparse Core Ops, SparseCore 0:
  9.7 27.8 all-gather.18
  39.3 25.9 all-gather.16
  67.0 25.9 all-gather.14
  94.5 88.0 all-gather.12
  184.1 87.2 all-gather.10
  309.4 87.5 reduce-scatter.3
where the time goes:
time: 405 us; the launch traced here: 404 us
  waiting for transfers between devices  305 us (75%)
  local copies, waits for them, and re-layouts  35.8 us (9%)
  blocking collectives  23.4 us (6%)
  matrix products  22.9 us (6%)
  between operations  14.9 us (4%)
    all_gather x1, waiting for transfers between devices, per_device(): full_in = whole_rows(lax.all_gather(inputs, TOK, axis=0))  86.8 us
    all_gather x1, waiting for transfers between devices, per_device(): full_cot = whole_rows(lax.all_gather(cotangent, TOK, axis=0))  82.3 us
    reduce_scatter x1, waiting for transfers between devices, per_device(): input_grad = lax.psum_scatter(blocks, TOK, scatter_dimension=0)  55.5 us
    all_gather x1, waiting for transfers between devices, per_device(): wg = lax.all_gather(gate_weight, HID, axis=0, tiled=True)  27 us
    all_gather x1, waiting for transfers between devices, per_device(): wu = lax.all_gather(up_weight, HID, axis=0, tiled=True)  25.8 us
    all_gather x1, waiting for transfers between devices, per_device(): wd = lax.all_gather(down_weight, HID, axis=0, tiled=True)  24.8 us
    unnamed x1, blocking collectives  23.4 us
    reshape x2, local copies, waits for them, and re-layouts, whole_rows(): halves = pieces.reshape(groups // 2, 2, rows, width)  13 us
  transfers between devices with their start and end apart: 7, of which 6 were waited for; matrix products, arithmetic and copies ran while one was open for 11% of the time, Pallas kernels for 0%

commit v1 on v0

--- a/solution.py
+++ b/solution.py
@@ -32,7 +32,10 @@
     rows, half = inputs.shape
     full_in = whole_rows(lax.all_gather(inputs, TOK, axis=0))
     full_cot = whole_rows(lax.all_gather(cotangent, TOK, axis=0))
-    wg = lax.all_gather(gate_weight, HID, axis=0, tiled=True)
+    devices = lax.axis_size(HID)
+    parts = jnp.stack([gate_weight for _ in range(devices)])
+    parts = lax.all_to_all(parts, HID, split_axis=0, concat_axis=0)
+    wg = jnp.concatenate(parts, axis=0)
     wu = lax.all_gather(up_weight, HID, axis=0, tiled=True)
     wd = lax.all_gather(down_weight, HID, axis=0, tiled=True)
     gate = rdot(full_in, wg)

time: 405 us -> 393 us (0.970)
  waiting for transfers between devices: 305 us -> 251 us
  blocking collectives: 23.4 us -> 66.2 us
    all_to_all x0 -> x1, blocking collectives: none -> 42.8 us  [per_device(): parts = lax.all_to_all(parts, HID, split_axis=0, concat_axis=0)]
    all_gather x1 -> x0, waiting for transfers between devices: 27 us -> none  [per_device(): wg = lax.all_gather(gate_weight, HID, axis=0, tiled=True)]
    all_gather x1, waiting for transfers between devices: 25.8 us -> 0.01 us  [per_device(): wu = lax.all_gather(up_weight, HID, axis=0, tiled=True)]
    unnamed x13 -> x12, local copies, waits for them, and re-layouts: 10 us -> 7.23 us
  transfers between devices with their start and end apart: 7 -> 6, of which waited for: 6 -> 4; matrix products, arithmetic and copies ran while one was open for 11% -> 11% of each run, Pallas kernels for 0% -> 0%
where the time goes in v1:
time: 393 us; the launch traced here: 392 us
  waiting for transfers between devices  251 us (64%)
  blocking collectives  66.2 us (17%)
  local copies, waits for them, and re-layouts  35.7 us (9%)
  matrix products  22.8 us (6%)
  between operations  14.5 us (4%)
    all_gather x1, waiting for transfers between devices, per_device(): full_in = whole_rows(lax.all_gather(inputs, TOK, axis=0))  86.8 us
    all_gather x1, waiting for transfers between devices, per_device(): full_cot = whole_rows(lax.all_gather(cotangent, TOK, axis=0))  82.3 us
    reduce_scatter x1, waiting for transfers between devices, per_device(): input_grad = lax.psum_scatter(blocks, TOK, scatter_dimension=0)  55.6 us
    all_to_all x1, blocking collectives, per_device(): parts = lax.all_to_all(parts, HID, split_axis=0, concat_axis=0)  42.8 us
    all_gather x1, waiting for transfers between devices, per_device(): wd = lax.all_gather(down_weight, HID, axis=0, tiled=True)  23.7 us
    unnamed x1, blocking collectives  23.4 us
    reshape x2, local copies, waits for them, and re-layouts, whole_rows(): halves = pieces.reshape(groups // 2, 2, rows, width)  13 us
    dot_general x3, matrix products, rdot(): lax.dot_general(left, right, (((1,), (1,)), ((), ())), preferred_element_...  10.4 us
  transfers between devices with their start and end apart: 6, of which 4 were waited for; matrix products, arithmetic and copies ran while one was open for 11% of the time, Pallas kernels for 0%

profile of v1, /device:TPU:2, one launch (start us, length us, event | category | flops | bytes accessed | tf_op | source)
XLA Modules:
  0.0 391.8 jit_solution(13469461599624406125)
XLA Ops:
  7.2 0.7 all-gather.15.cloned.1.call-update
  7.9 0.0 all-gather.13.cloned.1.call-start
  7.9 0.7 all-gather.13.cloned.1.call-update
  8.6 0.0 all-gather.11.cloned.1.call-start
  8.7 0.7 all-gather.11.cloned.1.call-update
  9.4 0.0 all-gather.9.cloned.1.call-start
  9.4 0.5 all-gather.9.cloned.1.call-update
  10.0 0.0 reduce-scatter.4.cloned.1.call-start
  10.0 1.1 stack.2
  11.1 42.8 %all_to_all.5 = bf16[8,74,1792]{2,1,0:T(8,128)(2,1)S(1)} all-to-all(bf16[8,74,1792]{2,1,0:T(8,128)(2,1)S(1)} %stack.2), channel_id=1, replica_groups=mesh['dp_0'=2,'dp_1'=4,'dp_2'=4,'dp_3'=2,'mp'=2] {'dp_2','dp_3'}, dimensions={0} | all-to-all | bytes 4243456 | tf_op jit(solution)/shard_map/all_to_all | solution.py:37
  53.9 1.6 reshape.31
  55.5 1.9 reshape.41
  57.4 23.7 %all-gather.13.cloned.1.call-done = bf16[8,74,1792]{2,1,0:T(8,128)(2,1)} async-done(((bf16[1,74,1792]{2,1,0:T(8,128)(2,1)}), bf16[8,74,1792]{2,1,0:T(8,128)(2,1)}) %all-gather.13.cloned.1.call-update) | async-done | bytes 2121744 | tf_op jit(solution)/shard_map/all_gather | solution.py:40
  81.1 3.0 reshape.39
  84.1 86.8 %all-gather.11.cloned.1.call-done = bf16[2048,896]{1,0:T(8,128)(2,1)} async-done(((bf16[128,896]{1,0:T(8,128)(2,1)}), bf16[2048,896]{1,0:T(8,128)(2,1)}) %all-gather.11.cloned.1.call-update) | async-done | bytes 3670032 | tf_op jit(solution)/shard_map/all_gather | solution.py:33
  170.9 6.5 %copy.12 = bf16[8,2,128,896]{2,0,3,1:T(8,128)(2,1)} copy(bf16[8,2,128,896]{3,2,1,0:T(8,128)(2,1)} %bitcast.43) | data formatting | bytes 7340032 | tf_op jit(solution)/shard_map/reshape | solution.py:27
  177.4 82.3 %all-gather.9.cloned.1.call-done = bf16[2048,896]{1,0:T(8,128)(2,1)} async-done(((bf16[128,896]{1,0:T(8,128)(2,1)}), bf16[2048,896]{1,0:T(8,128)(2,1)}) %all-gather.9.cloned.1.call-update) | async-done | bytes 3670032 | tf_op jit(solution)/shard_map/all_gather | solution.py:34
  259.7 6.5 %copy.11 = bf16[8,2,128,896]{2,0,3,1:T(8,128)(2,1)} copy(bf16[8,2,128,896]{3,2,1,0:T(8,128)(2,1)} %bitcast.47) | data formatting | bytes 7340032 | tf_op jit(solution)/shard_map/reshape | solution.py:27
  266.2 5.2 %fusion.7 = f32[1024,592]{0,1:T(8,128)S(1)} fusion(bf16[592,1792]{1,0:T(8,128)(2,1)} %reshape.39, bf16[224,8,8,128]{3,2,1,0:T(8,128)(2,1)} %bitcast.48), kind=kOutput, calls=%fused_computation.7 | convolution fusion | flops 2172649472 | bytes 8216576 | tf_op jit(solution)/shard_map/dot_general | solution.py:20
  271.4 2.4 fusion.5
  273.8 2.9 multiply_convert_fusion.1
  276.7 3.1 fusion.20
  279.8 4.8 %add_convert_fusion = bf16[1024,1792]{1,0:T(8,128)(2,1)} fusion(f32[1024,1792]{1,0:T(8,128)S(1)} %fusion.20, bf16[592,1792]{1,0:T(8,128)(2,1)S(1)} %reshape.41, f32[1024,592]{0,1:T(8,128)S(1)} %fusion.7, f32[1024,592]{0,1:T(8,128)S(1)} %fusion.5), kind=kOutput, calls=%fused_computation | convolution fusion | flops 2179956736 | bytes 17981440 | tf_op jit(solution)/shard_map/dot_general | solution.py:49
  284.6 8.1 %reshape.32 = bf16[8,128,2,896]{3,2,1,0:T(2,128)(2,1)} reshape(bf16[1024,1792]{1,0:T(8,128)(2,1)} %add_convert_fusion) | data formatting | bytes 7340032 | tf_op jit(solution)/shard_map/reshape | solution.py:50
  292.7 4.7 %copy.13 = bf16[8,2,128,896]{3,2,1,0:T(8,128)(2,1)} copy(bf16[8,2,128,896]{3,1,2,0:T(2,128)(2,1)} %bitcast.42) | data formatting | bytes 7340032 | tf_op jit(solution)/shard_map/transpose | solution.py:51
  297.4 4.4 %fusion.10 = bf16[592,1792]{1,0:T(8,128)(2,1)S(1)} fusion(bf16[1024,592]{0,1:T(8,128)(2,1)S(1)} %multiply_convert_fusion.1, bf16[224,8,8,128]{3,2,1,0:T(8,128)(2,1)} %bitcast.44), kind=kOutput, calls=%fused_computation.10 | convolution fusion | flops 2173710336 | bytes 7004160 | tf_op jit(solution)/shard_map/dot_general | solution.py:14
  301.9 23.4 %fusion = bf16[80,1792]{1,0:T(8,128)(2,1)S(1)} fusion(bf16[592,1792]{1,0:T(8,128)(2,1)S(1)} %fusion.10), kind=kCustom, calls=%all-reduce-scatter | all-reduce-scatter fusion | flops 1146881 | bytes 2408960
  325.3 1.3 collective-permute-start
  326.6 0.6 dynamic-slice.4
  327.9 0.9 concatenate
  328.8 0.8 constant_dynamic-slice_fusion
  329.6 55.6 %reduce-scatter.4.cloned.1.call-done = bf16[1,128,896]{2,1,0:T(8,128)(2,1)} async-done(((bf16[16,128,896]{2,1,0:T(8,128)(2,1)}), bf16[1,128,896]{2,1,0:T(8,128)(2,1)}) %reduce-scatter.4.cloned.1.call-update) | async-done | bytes 229392 | tf_op jit(solution)/shard_map/reduce_scatter | solution.py:52
  (11 shorter events, 0.1 us)
Async XLA Ops:
  7.2 48.4 %all-gather.15.cloned.1.call-start = ((), (), s32[]{:S(2)}) async-start(), calls=%async_computation.6 | async-start | bytes 2580480 | tf_op jit(solution)/shard_map/all_gather | solution.py:39
  7.9 73.2 %all-gather.13.cloned.1.call-start = ((), (), s32[]{:S(2)}) async-start(), calls=%async_computation.5 | async-start | bytes 2580480 | tf_op jit(solution)/shard_map/all_gather | solution.py:40
  8.6 162.2 %all-gather.11.cloned.1.call-start = ((), (), s32[]{:S(2)}) async-start(), calls=%async_computation.4 | async-start | bytes 3899392 | tf_op jit(solution)/shard_map/all_gather | solution.py:33
  9.4 250.3 %all-gather.9.cloned.1.call-start = ((), (), s32[]{:S(2)}) async-start(), calls=%async_computation.3 | async-start | bytes 3899392 | tf_op jit(solution)/shard_map/all_gather | solution.py:34
  10.0 375.3 %reduce-scatter.4.cloned.1.call-start = ((), (), s32[]{:S(2)}) async-start(), calls=%async_computation.2 | async-start | bytes 3899392 | tf_op jit(solution)/shard_map/reduce_scatter | solution.py:52
  266.2 5.2 %copy-start = (bf16[8,2,128,896]{2,0,3,1:T(8,128)(2,1)S(1)}, bf16[8,2,128,896]{2,0,3,1:T(8,128)(2,1)}, u32[]{:S(2)}) copy-start(bf16[8,2,128,896]{2,0,3,1:T(8,128)(2,1)} %copy.12) | copy-start | bytes 11010052
  266.2 5.2 %copy-start.1 = (bf16[592,1792]{1,0:T(8,128)(2,1)S(1)}, bf16[592,1792]{1,0:T(8,128)(2,1)}, u32[]{:S(2)}) copy-start(bf16[592,1792]{1,0:T(8,128)(2,1)} %reshape.31) | copy-start | bytes 6365188
  301.9 24.7 %copy-start.2 = (u32[128]{0:T(128)S(1)}, u32[128]{0:T(128)}, u32[]{:S(2)}) copy-start(u32[128]{0:T(128)} %constant.7) | copy-start | bytes 1540
  325.3 2.6 collective-permute-start
Sparse Core Ops, SparseCore 0:
  9.7 44.4 all-gather.14
  55.9 25.1 all-gather.12
  82.8 88.0 all-gather.10
  172.4 87.2 all-gather.8
  297.5 87.6 reduce-scatter.3
